TPU v7x, 128 devices: a whole 4x4x4 slice. The times are simulated.
128 devices in a mesh: dev: 32 (over y, x, core), ka: 4 (over z).
Axes of the slice: x: 4, y: 4, z: 4, core: 2. Of those that a mesh axis runs over, the one named last changes fastest.
Arguments:
- tile_data: float32 [8192, 128, 128], P(('dev', 'ka')), may hold values from -0.25 to 0.25
- tile_row: int32 [128, 64], P(('dev', 'ka')), may hold values from 0 to 31
- tile_col: int32 [128, 64], P(('dev', 'ka')), may hold values from 0 to 63
- tile_count: int32 [128], P(('dev', 'ka')), may hold values from 10 to 64, as said below
- touched: int32 [128, 64], P(('dev', 'ka')), may hold values from 0 to 511, as said below
- owner_map: int32 [512], replicated, may hold values from 0 to 511, as said below
- observed: float32 [4096, 128, 64], P(('dev', 'ka')), may hold values from -6 to 6
- start_x: float32 [8192, 128, 64], P(('dev', 'ka')), may hold values from -6 to 6
- start_u: float32 [8192, 128, 64], P(('dev', 'ka')), may hold values from -4 to 4
Outputs:
- final_x: float32 [8192, 128, 64], P(('dev', 'ka'))
- final_u: float32 [8192, 128, 64], P(('dev', 'ka'))
- z_keeper_agreed: float32 [512, 128, 64], P(('dev', 'ka'))
- primal_gap: float32 [64], replicated
Inputs may be any that keep to these rules, and one draw needn't show every extreme that they name: Shard s uses its first tile_count[s] slots; each count is at least 10 and at most 64, and some shard has exactly 64. `touched`: A shard's 64 entries are distinct column blocks. The owner of block j is shard owner_map[j] // 4; a shard touches at most one block of any one owner, and every shard touches exactly one block of some owner. `owner_map`: A permutation of 0 to 511.
All inputs are finite; a program needn't handle non-finite values.
Results may differ from a plain program's by a relative error of at most 0.0003.
Values sent between devices are 32-bit elements.
A program may use at most 128 MiB of HBM per device.

v0:
```python
import functools

import jax
import jax.numpy as jnp
from jax import lax
from jax.experimental import pallas as pl
from jax.experimental.pallas import tpu as pltpu
from jax.sharding import PartitionSpec as P

ITERS = 2
CG_STEPS = 4
PENALTY = 1.0
COUPLING = 1.0
AXES = ("dev", "ka")
MESH = pl.DeviceIdType.MESH
MIB = 1 << 20
VMEM_MIB = 61
PIECE = 8
ORDERS = ("zyx", "yxz", "xzy")
SLOT, MAIL, FWD_TILE, FWD_FROM, FWD_FIRST, BWD_TILE, BWD_FROM, BWD_FIRST, ROW_LAST, COL_LAST = (
    0, 3, 6, 7, 8, 9, 10, 11, 12, 13,
)


def split(value):
    high = value.astype(jnp.bfloat16)
    low = (value - high.astype(jnp.float32)).astype(jnp.bfloat16)
    return jnp.concatenate([high, low], axis=0)


def lanes(total):
    return jnp.sum(total, axis=1, keepdims=True)


def kernel(
    n, cb, mean_of,
    tab, tags_ref, tile_hbm, obs_hbm, x_hbm, u_hbm,
    x_ref, u_ref, zown_ref, gap_ref,
    tile_ref, obs_ref, fwd_ref, bwd_ref, pb_ref, wb_ref, wseg, qseg, r_ref, p_ref, zu_ref,
    box, in1, sum1, in2, sum2, in3, zz2, zz1, ans, zbox, tagin, tagx, share_ref, gin,
    load_sem, r1_s, r1_r, r2_s, r2_r, r3_s, r3_r, b3_s, b3_r, b2_s, b2_r, b1_s, b1_r,
    tag_s, tag_r, gap_s, gap_r,
):
    slots, blk, _ = tile_ref.shape
    local_cols, targets, _ = x_ref.shape
    row_blocks = obs_ref.shape[0]
    subs = targets // PIECE
    plane = n * n
    groups = 2 * n
    f32 = jnp.float32
    md, mk = lax.axis_index(AXES[0]), lax.axis_index(AXES[1])
    at = {"c": lax.rem(md, 2), "x": lax.rem(md // 2, n), "y": md // (2 * n), "z": mk}

    def device(axis, da, dc=0):
        place = dict(at)
        place[axis] = lax.rem(place[axis] + da, n)
        place["c"] = lax.rem(place["c"] + dc, 2)
        return ((place["y"] * n + place["x"]) * 2 + place["c"], place["z"])

    def remote(source, target, send_sem, recv_sem, where):
        return pltpu.make_async_remote_copy(
            source, target, send_sem, recv_sem, device_id=where, device_id_type=MESH
        )

    def order(k):
        return k % 3 if k < subs else 0

    def axis(k, level):
        return ORDERS[order(k)][level]

    def back(da):
        return (n - da) % n

    line = [(dc, da) for dc in range(2) for da in range(n)][1:]
    anyone = device("x", 1)

    def line_sends(k, p, source, target, send_sem, recv_sem):
        for dc, da in line:
            mine, theirs = (dc * n + da) * plane, (dc * n + back(da)) * plane
            remote(
                source.at[k, pl.ds(mine, plane)], target.at[k, pl.ds(theirs, plane)],
                send_sem.at[k], recv_sem.at[k], device(ORDERS[p][0], da, dc),
            ).start()

    def ring_sends(k, where, pick, size, source, target, send_sem, recv_sem):
        for da in range(1, n):
            remote(
                source.at[k, pl.ds(da * size if pick else 0, size)],
                target.at[k, pl.ds(back(da) * size, size)],
                send_sem.at[k], recv_sem.at[k], device(where, da),
            ).start()

    def rest(ref, k, size):
        return ref.at[k, pl.ds(size, ref.shape[1] - size)]

    def arrived(ref, k, size, sems):
        part = rest(ref, k, size)
        remote(part, part, sems[0].at[k], sems[1].at[k], anyone).wait_recv()

    def left(ref, k, size, sems):
        part = rest(ref, k, size)
        remote(part, part, sems[0].at[k], sems[1].at[k], anyone).wait_send()

    r1, r2, r3 = (r1_s, r1_r), (r2_s, r2_r), (r3_s, r3_r)
    b3, b2, b1 = (b3_s, b3_r), (b2_s, b2_r), (b1_s, b1_r)
    tagged = (tag_s, tag_r)

    greeted = [device(ORDERS[0][0], da, dc) for dc, da in line]
    for where in ORDERS[0][1:]:
        greeted += [device(where, da, dc) for dc in range(2) for da in range(1, n)]
    barrier = pltpu.get_barrier_semaphore()
    for where in greeted:
        pl.semaphore_signal(barrier, inc=1, device_id=where, device_id_type=MESH)

    loads = [
        pltpu.make_async_copy(source, target, load_sem.at[i])
        for i, (source, target) in enumerate(
            ((x_hbm, x_ref), (u_hbm, u_ref), (tile_hbm, tile_ref), (obs_hbm, obs_ref))
        )
    ]
    for one in loads:
        one.start()

    def members(p):
        return [k for k in range(subs) if order(k) == p]

    def build(p):
        def one(i, carry):
            for g in range(groups):
                q = g * plane + i
                slot = tab[SLOT + p, q]
                for k in members(p):
                    rows = pl.ds(k * PIECE, PIECE)
                    box[k, q] = x_ref[slot, rows] + u_ref[slot, rows]
            return carry

        lax.fori_loop(0, plane, one, 0)

    def send_r1(k):
        line_sends(k, order(k), box, in1, *r1)

    def send_r2(k):
        ring_sends(k, axis(k, 1), True, n * cb, sum1, in2, *r2)

    def t1(k):
        p = order(k)
        arrived(in1, k, plane, r1)

        def one(i, carry):
            total = [jnp.zeros((PIECE, blk), f32)] * cb
            for s in range(groups):
                value = box[k, i] if s == 0 else in1[k, s * plane + i]
                tag = tagx[p, i * groups + s]
                total = [t + jnp.where(tag == b, value, 0.0) for b, t in enumerate(total)]
            for b in range(cb):
                sum1[k, i * cb + b] = total[b]
            return carry

        lax.fori_loop(0, plane, one, 0, unroll=2)
        send_r2(k)

    def t2(k):
        size = n * cb
        arrived(in2, k, size, r2)
        for j in range(size):
            total = sum1[k, j]
            for s in range(1, n):
                total = total + in2[k, s * size + j]
            sum2[k, j] = total
        ring_sends(k, axis(k, 2), True, cb, sum2, in3, *r3)

    def total3(k, b):
        total = sum2[k, b]
        for s in range(1, n):
            total = total + in3[k, s * cb + b]
        return total

    def t3(k):
        arrived(in3, k, cb, r3)
        for b in range(cb):
            share = share_ref[b]
            amount = total3(k, b) / share
            cutoff = PENALTY / (COUPLING * share)
            z = amount - jnp.clip(amount, -cutoff, cutoff)
            zz2[k, b] = z
            zown_ref[b, pl.ds(k * PIECE, PIECE)] = z
        ring_sends(k, axis(k, 2), False, cb, zz2, zz2, *b3)

    def t4(k):
        arrived(zz2, k, cb, b3)
        for j in range(n * cb):
            zz1[k, j] = zz2[k, j]
        ring_sends(k, axis(k, 1), False, n * cb, zz2, zz1, *b2)

    def t5(k):
        p = order(k)
        arrived(zz1, k, n * cb, b2)

        def one(i, carry):
            z = [zz1[k, i * cb + b] for b in range(cb)]
            for s in range(groups):
                tag = tagx[p, i * groups + s]
                value = z[cb - 1]
                for b in range(cb - 1):
                    value = jnp.where(tag == b, z[b], value)
                if s == 0:
                    zbox[k, i] = value
                else:
                    ans[k, s * plane + i] = value
            return carry

        lax.fori_loop(0, plane, one, 0, unroll=2)
        line_sends(k, p, ans, zbox, *b1)

    waves = [list(range(f, min(f + 3, subs))) for f in range(0, subs, 3)]

    def start_exchange():
        for p in range(3):
            build(p)

    def exchange(first):
        last = len(waves) - 1
        if first:
            t2(subs)
        for tick in range(2 * last + 5):
            for level, task in ((5, t5), (4, t4), (3, t3), (2, t2), (1, t1)):
                late = tick - (level - 1)
                if late < 0 or late % 2:
                    continue
                w = late // 2
                if w > last:
                    continue
                for k in waves[w]:
                    task(k)
                    if level == 1 and k + 6 < subs:
                        send_r1(k + 6)
            if first and tick == 0:
                arrived(in3, subs, cb, r3)
                for b in range(cb):
                    share_ref[b] = jnp.maximum(total3(subs, b), 1.0)
        for k in range(subs):
            arrived(zbox, k, plane, b1)
        for k in range(subs + 1 if first else subs):
            left(sum1, k, n * cb, r2)
            left(sum2, k, cb, r3)
        for k in range(subs):
            left(box, k, plane, r1)
            left(in3, k, cb, b3)
            left(zz1, k, n * cb, b2)
            left(ans, k, plane, b1)

    def tile_pass(tiles_ref, from_row, first_row, source_ref, seg_ref):
        group = min(16, slots)

        def step(number, total):
            for inner in range(group):
                t = number * group + inner
                lhs = source_ref[tab[from_row, t]]
                out = jnp.dot(
                    jnp.concatenate([lhs, lhs], axis=1), tiles_ref[t],
                    preferred_element_type=f32,
                )
                fresh = tab[first_row, t] == 1
                total = jnp.where(fresh, 0.0, total) + (out[:targets] + out[targets:])
                seg_ref[t] = total
            return total

        lax.fori_loop(0, slots // group, step, jnp.zeros((targets, blk), f32))

    def forward():
        tile_pass(fwd_ref, FWD_FROM, FWD_FIRST, pb_ref, wseg)

    def backward():
        tile_pass(bwd_ref, BWD_FROM, BWD_FIRST, wb_ref, qseg)

    def loop(count, body, init=0, unroll=4):
        return lax.fori_loop(0, count, body, init, unroll=unroll)

    zero = jnp.zeros((targets, blk), f32)
    wseg[slots] = zero
    qseg[slots] = zero

    loads[0].wait()
    loads[1].wait()
    start_exchange()
    pl.semaphore_wait(barrier, len(greeted))
    for p in range(3):
        line_sends(p, p, tags_ref, tagin, *tagged)
    for k in range(min(6, subs)):
        send_r1(k)

    def opening(c, carry):
        pb_ref[c] = split(x_ref[c])
        return carry

    loop(local_cols, opening)
    loads[2].wait()

    def convert(t, carry):
        fwd_ref[t] = split(tile_ref[tab[FWD_TILE, t]].T)
        bwd_ref[t] = split(tile_ref[tab[BWD_TILE, t]])
        return carry

    loop(slots, convert)

    for p in range(3):
        arrived(tagin, p, plane, tagged)
        left(tagin, p, plane, tagged)

        def expand(i, carry):
            for s in range(groups):
                q = s * plane + i
                row = (tags_ref if s == 0 else tagin)[p, pl.ds(q, 1)]
                tagx[p, i * groups + s] = jnp.broadcast_to(row, (PIECE, blk))
            return carry

        loop(plane, expand, unroll=1)

    def census(i, carry):
        total = [jnp.zeros((PIECE, blk), f32)] * cb
        for s in range(groups):
            tag = tagx[0, i * groups + s]
            total = [t + jnp.where(tag == b, 1.0, 0.0) for b, t in enumerate(total)]
        for b in range(cb):
            sum1[subs, i * cb + b] = total[b]
        return carry

    loop(plane, census, unroll=1)
    send_r2(subs)

    forward()
    loads[3].wait()

    def against(r, carry):
        wb_ref[r] = split(obs_ref[r] - wseg[tab[ROW_LAST, r]])
        return carry

    loop(row_blocks, against)
    backward()

    def basis(c, carry):
        r_ref[c] = qseg[tab[COL_LAST, c]] - COUPLING * x_ref[c]
        return carry

    loop(local_cols, basis)
    exchange(True)

    gap_line = ORDERS[0]

    def gap_send(stage):
        if stage == 0:
            for dc, da in line:
                remote(
                    gin.at[0, pl.ds(0, 1)], gin.at[0, pl.ds(dc * n + back(da), 1)],
                    gap_s.at[0], gap_r.at[0], device(gap_line[0], da, dc),
                ).start()
        else:
            ring_sends(stage, gap_line[stage], False, 1, gin, gin, gap_s, gap_r)

    def gap_total(stage):
        count = groups if stage == 0 else n
        part = gin.at[stage, pl.ds(1, count - 1)]
        one = remote(part, part, gap_s.at[stage], gap_r.at[stage], anyone)
        one.wait_recv()
        one.wait_send()
        total = gin[stage, 0]
        for s in range(1, count):
            total = total + gin[stage, s]
        return total

    for outer_step in range(ITERS):
        last = outer_step == ITERS - 1

        def begin(c, carry):
            rr, gap = carry
            z = jnp.concatenate(
                [zbox[k, tab[MAIL + order(k), c]] for k in range(subs)], axis=0
            )
            d = x_ref[c] - z
            u = u_ref[c] + d
            u_ref[c] = u
            zu = z - u
            r = r_ref[c] + COUPLING * zu
            r_ref[c] = r
            p_ref[c] = r
            pb_ref[c] = split(r)
            if last:
                gap = gap + d * d
            else:
                zu_ref[c] = zu
            return rr + r * r, gap

        rr, gap = loop(local_cols, begin, (zero, zero), unroll=2)
        rr = lanes(rr)
        pp = rr
        if last:
            gin[0, 0] = lax.dot_general(
                jnp.ones((PIECE, blk), f32),
                jnp.concatenate([gap, jnp.zeros((blk - targets, blk), f32)], axis=0),
                (((1,), (1,)), ((), ())),
                precision=lax.Precision.HIGHEST, preferred_element_type=f32,
            )
            gap_send(0)

        for step in range(CG_STEPS):
            closing = step == CG_STEPS - 1
            forward()

            def image(i, ww):
                w = wseg[tab[ROW_LAST, i]]
                if not (last and closing):
                    wb_ref[i] = split(w)
                return ww + w * w

            ww = lanes(loop(row_blocks, image, zero))
            size = rr / (ww + COUPLING * pp)
            if closing:

                def finish(c, carry):
                    x_ref[c] = x_ref[c] + size * p_ref[c]
                    return carry

                loop(local_cols, finish)
                if last:
                    break
                start_exchange()
                for k in range(min(6, subs)):
                    send_r1(k)
                backward()

                def close(c, carry):
                    q = qseg[tab[COL_LAST, c]] + COUPLING * p_ref[c]
                    r_ref[c] = r_ref[c] - size * q - COUPLING * zu_ref[c]
                    return carry

                loop(local_cols, close)
                exchange(False)
                break
            backward()
            if last and step < 2:
                gin[step + 1, 0] = gap_total(step)
                gap_send(step + 1)

            def reduce(c, total):
                q = qseg[tab[COL_LAST, c]] + COUPLING * p_ref[c]
                r = r_ref[c] - size * q
                r_ref[c] = r
                return total + r * r

            norm = lanes(loop(local_cols, reduce, zero))
            turn = norm / rr

            def direct(c, total):
                old = p_ref[c]
                x_ref[c] = x_ref[c] + size * old
                p = r_ref[c] + turn * old
                p_ref[c] = p
                pb_ref[c] = split(p)
                return total + p * p

            pp = lanes(loop(local_cols, direct, zero, unroll=2))
            rr = norm
    gap_ref[...] = jnp.sqrt(gap_total(2) / mean_of)


def on_device(
    tile_data, tile_row, tile_col, tile_count, touched, owner_map, observed, start_x, start_u
):
    nd, n = lax.axis_size(AXES[0]), lax.axis_size(AXES[1])
    shards = nd * n
    local_cols = touched.shape[1]
    col_blocks = owner_map.shape[0]
    cb = col_blocks // shards
    row_blocks = observed.shape[0]
    slots, blk, _ = tile_data.shape
    targets = start_x.shape[2]
    subs = targets // PIECE
    f32, b16, i32 = jnp.float32, jnp.bfloat16, jnp.int32
    shape = jax.ShapeDtypeStruct
    assert nd == 2 * n * n and shards == 128 and col_blocks == cb * shards
    assert max(local_cols, slots, row_blocks) <= blk and targets % PIECE == 0

    md, mk = lax.axis_index(AXES[0]), lax.axis_index(AXES[1])
    wanted = touched[0]
    matches = wanted[:, None] == jnp.arange(col_blocks, dtype=i32)[None, :]
    position = jnp.sum(jnp.where(matches, owner_map[None, :], 0), axis=1)
    owner = position // cb
    local_slot = position - owner * cb
    away = {
        "z": (owner % n - mk) % n,
        "x": ((owner // (2 * n)) % n - (md // 2) % n) % n,
        "y": (owner // (2 * n * n) - md // (2 * n)) % n,
    }
    core = (owner // n + md) % 2
    mail = jnp.stack(
        [((core * n + away[a]) * n + away[b]) * n + away[c] for a, b, c in ORDERS]
    )
    hit = mail[:, :, None] == jnp.arange(shards, dtype=i32)[None, None, :]
    column = jnp.arange(local_cols, dtype=i32)
    slot_of = jnp.sum(jnp.where(hit, column[None, :, None], 0), axis=1)
    tags = jnp.sum(jnp.where(hit, local_slot[None, :, None] + 1, 0), axis=1) - 1
    tags = jnp.broadcast_to(tags.astype(f32)[:, :, None], (3, shards, blk))

    number = jnp.arange(slots, dtype=i32)
    used = number < tile_count[0]

    def sorting(keys, values, bins):
        keys = jnp.where(used, keys, bins)
        full = keys * slots + number
        before = full[None, :] < full[:, None]
        rank = jnp.sum(before.astype(i32), axis=1)
        same = before & (keys[None, :] == keys[:, None])
        first = 1 - jnp.max(same.astype(i32), axis=1)
        landed = rank[None, :] == number[:, None]
        pick = lambda v: jnp.sum(jnp.where(landed, v[None, :], 0), axis=1)
        bin_of = jnp.arange(bins, dtype=i32)
        upto = jnp.sum((keys[None, :] <= bin_of[:, None]).astype(i32), axis=1)
        some = jnp.max((keys[None, :] == bin_of[:, None]).astype(i32), axis=1)
        return pick(number), pick(values), pick(first), jnp.where(some > 0, upto - 1, slots)

    row, col = tile_row[0], tile_col[0]
    ftile, ffrom, ffirst, row_last = sorting(row, col, row_blocks)
    btile, bfrom, bfirst, col_last = sorting(col, row, local_cols)

    def padded(v):
        return jnp.pad(v, (0, blk - v.shape[0]))[None, :]

    table = jnp.concatenate(
        [slot_of, jnp.pad(mail, ((0, 0), (0, blk - local_cols)))]
        + [padded(v) for v in (ftile, ffrom, ffirst, btile, bfrom, bfirst, row_last, col_last)],
        axis=0,
    )

    x = jnp.swapaxes(start_x, 1, 2)
    u = jnp.swapaxes(start_u, 1, 2)
    obs = jnp.swapaxes(observed, 1, 2)
    vec = (local_cols, targets, blk)
    pieces = lambda *lead: pltpu.VMEM((*lead, PIECE, blk), f32)
    dma = lambda *count: pltpu.SemaphoreType.DMA(count)
    plane, groups, ring = n * n, 2 * n, n * cb
    vm = pl.BlockSpec(memory_space=pltpu.VMEM)
    hbm = pl.BlockSpec(memory_space=pltpu.HBM)
    x, u, zown, gap = pl.pallas_call(
        functools.partial(kernel, n, cb, shards * local_cols * blk),
        out_shape=(
            shape(vec, f32), shape(vec, f32), shape((cb, targets, blk), f32),
            shape((PIECE, blk), f32),
        ),
        in_specs=[pl.BlockSpec(memory_space=pltpu.SMEM), vm, hbm, hbm, hbm, hbm],
        out_specs=(vm,) * 4,
        scratch_shapes=[
            pltpu.VMEM((slots, blk, blk), f32),
            pltpu.VMEM((row_blocks, targets, blk), f32),
            pltpu.VMEM((slots, 2 * blk, blk), b16),
            pltpu.VMEM((slots, 2 * blk, blk), b16),
            pltpu.VMEM((local_cols, 2 * targets, blk), b16),
            pltpu.VMEM((row_blocks, 2 * targets, blk), b16),
            pltpu.VMEM((slots + 1, targets, blk), f32),
            pltpu.VMEM((slots + 1, targets, blk), f32),
            pltpu.VMEM(vec, f32), pltpu.VMEM(vec, f32), pltpu.VMEM(vec, f32),
            pieces(subs, shards), pieces(subs, shards),
            pieces(subs + 1, plane * cb), pieces(subs + 1, plane * cb),
            pieces(subs + 1, ring), pieces(subs + 1, ring),
            pieces(subs, ring), pieces(subs, plane * cb),
            pieces(subs, shards), pieces(subs, shards),
            pltpu.VMEM((3, shards, blk), f32), pieces(3, shards),
            pieces(cb), pieces(3, groups),
            dma(4), dma(subs), dma(subs),
            dma(subs + 1), dma(subs + 1), dma(subs + 1), dma(subs + 1),
            dma(subs), dma(subs), dma(subs), dma(subs), dma(subs), dma(subs),
            dma(3), dma(3), dma(3), dma(3),
        ],
        compiler_params=pltpu.CompilerParams(
            vmem_limit_bytes=VMEM_MIB * MIB, has_side_effects=True, collective_id=0
        ),
        name="admm",
    )(table, tags, tile_data, obs, x, u)
    primal_gap = gap[0, :targets]
    return (jnp.swapaxes(x, 1, 2), jnp.swapaxes(u, 1, 2), jnp.swapaxes(zown, 1, 2), primal_gap)


def solution(mesh):
    both = P(AXES)
    placed = (
        P(AXES, None, None), P(AXES, None), P(AXES, None), both, P(AXES, None), P(),
        P(AXES, None, None), P(AXES, None, None), P(AXES, None, None),
    )
    return jax.shard_map(
        on_device,
        mesh=mesh,
        in_specs=placed,
        out_specs=(P(AXES, None, None), P(AXES, None, None), P(AXES, None, None), P()),
        check_vma=False,
    )
```

profile of v0, /device:TPU:1, one launch (start us, length us, event | category | flops | bytes accessed | tf_op | source)
XLA Modules:
  0.0 212.0 jit_solution(12771783114230996026)
XLA Ops:
  1.3 0.9 select_reduce_fusion
  2.3 0.1 select_reduce_fusion.1
  2.4 0.7 iota_add_fusion
  3.1 0.7 add_bitcast_fusion
  3.8 0.2 convert_reduce_fusion
  4.0 0.2 convert_reduce_fusion.3
  4.2 0.8 select_reduce_fusion.3
  5.0 0.8 select_reduce_fusion.6
  5.9 0.1 convert_reduce_fusion.4
  6.0 1.2 concatenate.3.tab
  7.2 0.8 broadcast_in_dim.164.tags_ref
  8.0 197.5 %admm.1 = (f32[64,64,128]{2,1,0:T(8,128)}, f32[64,64,128]{2,1,0:T(8,128)}, f32[4,64,128]{2,1,0:T(8,128)}, f32[8,128]{1,0:T(8,128)}) custom-call(s32[14,128]{1,0:T(8,128)} %concatenate.3.tab, f32[3,128,128]{2,1,0:T(8,128)} %broadcast_in_dim.164.tags_ref, f32[64,128,128]{2,1,0:T(8,128)} %tile_hbm.1, f32[32,64,128]{2,1,0:T(8,128)} %bitcast.106, ...), custom_call_target="tpu_custom_call" | custom-call | tf_op jit(solution)/shard_map/admm/pallas_call | solution.py:543
  205.5 1.2 slice_bitcast_fusion
  206.7 0.0 copy-start
  206.7 3.3 %copy.17 = f32[64,128,64]{1,2,0:T(8,128)} copy(f32[64,128,64]{1,2,0:T(8,128)} %bitcast.103) | data formatting | bytes 4194304
  210.0 0.0 copy-done
  210.0 0.0 copy-start.1
  210.0 1.3 copy.18
  211.4 0.0 copy-done.1
  211.4 0.7 copy.19
  (17 shorter events, 0.1 us)
Async XLA Ops:
  206.7 3.3 %copy-start = (f32[64,64,128]{2,1,0:T(8,128)S(1)}, f32[64,64,128]{2,1,0:T(8,128)}, u32[]{:S(2)}) copy-start(f32[64,64,128]{2,1,0:T(8,128)} %get-tuple-element.9) | copy-start | bytes 6291460
  210.0 1.3 copy-start.1
where the time goes:
time: 212 us
  Pallas kernels  197 us (93%)
  local copies, waits for them, and re-layouts  8.52 us (4%)
  other arithmetic  4.54 us (2%)
    pallas_call x1, Pallas kernels, on_device(): pl.pallas_call(functools.partial(kernel, n, cb, shards * local_cols * blk...  197 us
    unnamed x7, local copies, waits for them, and re-layouts  5.29 us

commit v1 on v0

--- a/solution.py
+++ b/solution.py
@@ -14,11 +14,23 @@
 AXES = ("dev", "ka")
 MESH = pl.DeviceIdType.MESH
 MIB = 1 << 20
-VMEM_MIB = 61
+VMEM_MIB = 48
 PIECE = 8
-ORDERS = ("zyx", "yxz", "xzy")
+ORDERS = ("xzy", "yxz", "zyx", "yzx")
+SUB_ORDER = (0, 1, 2, 0, 1, 2, 0, 3)
+KINDS = len(ORDERS)
 SLOT, MAIL, FWD_TILE, FWD_FROM, FWD_FIRST, BWD_TILE, BWD_FROM, BWD_FIRST, ROW_LAST, COL_LAST = (
-    0, 3, 6, 7, 8, 9, 10, 11, 12, 13,
+    0, 4, 8, 9, 10, 11, 12, 13, 14, 15,
+)
+FIRST_PLAN = (
+    7, 3, 6, 5, 1, 90, 2, 4, 0, 13, 91, 17, 15, 11, 92, 16, 12, 93, 14, 10, 25, 27, 21, 26,
+    23, 22, 24, 20, 35, 31, 36, 37, 33, 32, 34, 30, 45, 41, 46, 44, 42, 43, 40, 47, 51, 56,
+    52, 54, 50, 57, 55, 53,
+)
+NEXT_PLAN = (
+    0, 4, 5, 90, 7, 2, 3, 10, 1, 6, 15, 17, 14, 13, 12, 16, 11, 24, 20, 23, 25, 27, 22, 21,
+    26, 30, 34, 35, 33, 37, 32, 31, 36, 44, 40, 45, 41, 43, 42, 47, 46, 54, 50, 51, 55, 53,
+    52, 57, 56,
 )
 
 
@@ -37,9 +49,9 @@
     tab, tags_ref, tile_hbm, obs_hbm, x_hbm, u_hbm,
     x_ref, u_ref, zown_ref, gap_ref,
     tile_ref, obs_ref, fwd_ref, bwd_ref, pb_ref, wb_ref, wseg, qseg, r_ref, p_ref, zu_ref,
-    box, in1, sum1, in2, sum2, in3, zz2, zz1, ans, zbox, tagin, tagx, share_ref, gin,
+    box, in1, sum1, in2, sum2, in3, zz2, zz1, zbox, tagin, tagx, share_ref, gin, cin,
     load_sem, r1_s, r1_r, r2_s, r2_r, r3_s, r3_r, b3_s, b3_r, b2_s, b2_r, b1_s, b1_r,
-    tag_s, tag_r, gap_s, gap_r,
+    tag_s, tag_r, gap_s, gap_r, cnt_s, cnt_r,
 ):
     slots, blk, _ = tile_ref.shape
     local_cols, targets, _ = x_ref.shape
@@ -63,7 +75,7 @@
         )
 
     def order(k):
-        return k % 3 if k < subs else 0
+        return SUB_ORDER[k]
 
     def axis(k, level):
         return ORDERS[order(k)][level]
@@ -195,6 +207,7 @@
     def t5(k):
         p = order(k)
         arrived(zz1, k, n * cb, b2)
+        left(box, k, plane, r1)
 
         def one(i, carry):
             z = [zz1[k, i * cb + b] for b in range(cb)]
@@ -206,48 +219,32 @@
                 if s == 0:
                     zbox[k, i] = value
                 else:
-                    ans[k, s * plane + i] = value
+                    box[k, s * plane + i] = value
             return carry
 
         lax.fori_loop(0, plane, one, 0, unroll=2)
-        line_sends(k, p, ans, zbox, *b1)
-
-    waves = [list(range(f, min(f + 3, subs))) for f in range(0, subs, 3)]
+        line_sends(k, p, box, zbox, *b1)
 
     def start_exchange():
-        for p in range(3):
+        for p in range(KINDS):
             build(p)
 
-    def exchange(first):
-        last = len(waves) - 1
-        if first:
-            t2(subs)
-        for tick in range(2 * last + 5):
-            for level, task in ((5, t5), (4, t4), (3, t3), (2, t2), (1, t1)):
-                late = tick - (level - 1)
-                if late < 0 or late % 2:
-                    continue
-                w = late // 2
-                if w > last:
-                    continue
-                for k in waves[w]:
-                    task(k)
-                    if level == 1 and k + 6 < subs:
-                        send_r1(k + 6)
-            if first and tick == 0:
-                arrived(in3, subs, cb, r3)
-                for b in range(cb):
-                    share_ref[b] = jnp.maximum(total3(subs, b), 1.0)
+    def exchange(plan, works):
+        tasks = (send_r1, t1, t2, t3, t4, t5)
+        for step in plan:
+            level, k = divmod(step, 10)
+            if level == 9:
+                works[k]()
+            else:
+                tasks[level](k)
         for k in range(subs):
             arrived(zbox, k, plane, b1)
-        for k in range(subs + 1 if first else subs):
+        for k in range(subs):
             left(sum1, k, n * cb, r2)
             left(sum2, k, cb, r3)
-        for k in range(subs):
-            left(box, k, plane, r1)
             left(in3, k, cb, b3)
             left(zz1, k, n * cb, b2)
-            left(ans, k, plane, b1)
+            left(box, k, plane, b1)
 
     def tile_pass(tiles_ref, from_row, first_row, source_ref, seg_ref):
         group = min(16, slots)
@@ -284,66 +281,94 @@
     loads[1].wait()
     start_exchange()
     pl.semaphore_wait(barrier, len(greeted))
-    for p in range(3):
-        line_sends(p, p, tags_ref, tagin, *tagged)
-    for k in range(min(6, subs)):
-        send_r1(k)
-
-    def opening(c, carry):
-        pb_ref[c] = split(x_ref[c])
-        return carry
-
-    loop(local_cols, opening)
-    loads[2].wait()
-
-    def convert(t, carry):
-        fwd_ref[t] = split(tile_ref[tab[FWD_TILE, t]].T)
-        bwd_ref[t] = split(tile_ref[tab[BWD_TILE, t]])
-        return carry
-
-    loop(slots, convert)
-
-    for p in range(3):
-        arrived(tagin, p, plane, tagged)
-        left(tagin, p, plane, tagged)
-
-        def expand(i, carry):
+    for p in range(KINDS):
+        for dc, da in line:
+            remote(
+                tags_ref.at[p, pl.ds(dc * n + da, 1)],
+                tagin.at[p, pl.ds(dc * n + back(da), 1)],
+                tag_s.at[p], tag_r.at[p], device(ORDERS[p][0], da, dc),
+            ).start()
+
+    lane = lax.broadcasted_iota(jnp.int32, (PIECE, blk), 1)
+
+    def count_send(stage):
+        ring_sends(stage, ORDERS[0][stage + 1], False, 1, cin, cin, cnt_s, cnt_r)
+
+    def count_total(stage, size):
+        arrived(cin, stage, 1, (cnt_s, cnt_r))
+        left(cin, stage, 1, (cnt_s, cnt_r))
+        total = cin[stage, 0]
+        for s in range(1, n):
+            total = total + pltpu.roll(cin[stage, s], blk - back(s) * size, 1)
+        return total
+
+    def learn():
+        for p in range(KINDS):
+            tagin[p, 0] = tags_ref[p, 0]
+            arrived(tagin, p, 1, tagged)
+            left(tagin, p, 1, tagged)
+
+            def expand(s, carry):
+                row = tagin[p, s]
+                for i in range(plane):
+                    tagx[p, i * groups + s] = jnp.broadcast_to(row[:, i : i + 1], (PIECE, blk))
+                return carry
+
+            loop(groups, expand, unroll=1)
+
+        def census(i, held):
+            total = [jnp.zeros((PIECE, blk), f32)] * cb
             for s in range(groups):
-                q = s * plane + i
-                row = (tags_ref if s == 0 else tagin)[p, pl.ds(q, 1)]
-                tagx[p, i * groups + s] = jnp.broadcast_to(row, (PIECE, blk))
+                tag = tagx[0, i * groups + s]
+                total = [t + jnp.where(tag == b, 1.0, 0.0) for b, t in enumerate(total)]
+            for b in range(cb):
+                held = jnp.where(lane == i * cb + b, total[b], held)
+            return held
+
+        cin[0, 0] = loop(plane, census, jnp.zeros((PIECE, blk), f32), unroll=1)
+        count_send(0)
+
+    def ready():
+        def opening(c, carry):
+            pb_ref[c] = split(x_ref[c])
             return carry
 
-        loop(plane, expand, unroll=1)
-
-    def census(i, carry):
-        total = [jnp.zeros((PIECE, blk), f32)] * cb
-        for s in range(groups):
-            tag = tagx[0, i * groups + s]
-            total = [t + jnp.where(tag == b, 1.0, 0.0) for b, t in enumerate(total)]
+        loop(local_cols, opening)
+        loads[2].wait()
+
+        def convert(t, carry):
+            fwd_ref[t] = split(tile_ref[tab[FWD_TILE, t]].T)
+            bwd_ref[t] = split(tile_ref[tab[BWD_TILE, t]])
+            return carry
+
+        loop(slots, convert)
+        cin[1, 0] = count_total(0, n * cb)
+        count_send(1)
+
+    def towards():
+        forward()
+        loads[3].wait()
+
+        def against(r, carry):
+            wb_ref[r] = split(obs_ref[r] - wseg[tab[ROW_LAST, r]])
+            return carry
+
+        loop(row_blocks, against)
+        total = count_total(1, cb)
         for b in range(cb):
-            sum1[subs, i * cb + b] = total[b]
-        return carry
-
-    loop(plane, census, unroll=1)
-    send_r2(subs)
-
-    forward()
-    loads[3].wait()
-
-    def against(r, carry):
-        wb_ref[r] = split(obs_ref[r] - wseg[tab[ROW_LAST, r]])
-        return carry
-
-    loop(row_blocks, against)
-    backward()
-
-    def basis(c, carry):
-        r_ref[c] = qseg[tab[COL_LAST, c]] - COUPLING * x_ref[c]
-        return carry
-
-    loop(local_cols, basis)
-    exchange(True)
+            share = jnp.maximum(total[:, b : b + 1], 1.0)
+            share_ref[b] = jnp.broadcast_to(share, (PIECE, blk))
+
+    def basis():
+        backward()
+
+        def one(c, carry):
+            r_ref[c] = qseg[tab[COL_LAST, c]] - COUPLING * x_ref[c]
+            return carry
+
+        loop(local_cols, one)
+
+    exchange(FIRST_PLAN, (learn, ready, towards, basis))
 
     gap_line = ORDERS[0]
 
@@ -424,17 +449,18 @@
                 if last:
                     break
                 start_exchange()
-                for k in range(min(6, subs)):
-                    send_r1(k)
-                backward()
-
-                def close(c, carry):
-                    q = qseg[tab[COL_LAST, c]] + COUPLING * p_ref[c]
-                    r_ref[c] = r_ref[c] - size * q - COUPLING * zu_ref[c]
-                    return carry
-
-                loop(local_cols, close)
-                exchange(False)
+
+                def rest_of_step():
+                    backward()
+
+                    def close(c, carry):
+                        q = qseg[tab[COL_LAST, c]] + COUPLING * p_ref[c]
+                        r_ref[c] = r_ref[c] - size * q - COUPLING * zu_ref[c]
+                        return carry
+
+                    loop(local_cols, close)
+
+                exchange(NEXT_PLAN, (rest_of_step,))
                 break
             backward()
             if last and step < 2:
@@ -461,6 +487,18 @@
             pp = lanes(loop(local_cols, direct, zero, unroll=2))
             rr = norm
     gap_ref[...] = jnp.sqrt(gap_total(2) / mean_of)
+
+
+def deliver_kernel(x_ref, u_ref, z_ref, gap_ref, x_hbm, u_hbm, z_hbm, out_ref, sems):
+    copies = [
+        pltpu.make_async_copy(source, target, sems.at[i])
+        for i, (source, target) in enumerate(((x_ref, x_hbm), (u_ref, u_hbm), (z_ref, z_hbm)))
+    ]
+    for one in copies:
+        one.start()
+    out_ref[...] = gap_ref[0, : out_ref.shape[0]]
+    for one in copies:
+        one.wait()
 
 
 def on_device(
@@ -475,9 +513,10 @@
     slots, blk, _ = tile_data.shape
     targets = start_x.shape[2]
     subs = targets // PIECE
+    plane, groups, ring = n * n, 2 * n, n * cb
     f32, b16, i32 = jnp.float32, jnp.bfloat16, jnp.int32
     shape = jax.ShapeDtypeStruct
-    assert nd == 2 * n * n and shards == 128 and col_blocks == cb * shards
+    assert nd == 2 * n * n and shards == 128 and subs == len(SUB_ORDER)
     assert max(local_cols, slots, row_blocks) <= blk and targets % PIECE == 0
 
     md, mk = lax.axis_index(AXES[0]), lax.axis_index(AXES[1])
@@ -499,7 +538,9 @@
     column = jnp.arange(local_cols, dtype=i32)
     slot_of = jnp.sum(jnp.where(hit, column[None, :, None], 0), axis=1)
     tags = jnp.sum(jnp.where(hit, local_slot[None, :, None] + 1, 0), axis=1) - 1
-    tags = jnp.broadcast_to(tags.astype(f32)[:, :, None], (3, shards, blk))
+    tags = tags.astype(f32).reshape(KINDS, groups, 1, plane)
+    tags = jnp.pad(tags, ((0, 0), (0, 0), (0, 0), (0, blk - plane)))
+    tags = jnp.broadcast_to(tags, (KINDS, groups, PIECE, blk))
 
     number = jnp.arange(slots, dtype=i32)
     used = number < tile_count[0]
@@ -537,7 +578,6 @@
     vec = (local_cols, targets, blk)
     pieces = lambda *lead: pltpu.VMEM((*lead, PIECE, blk), f32)
     dma = lambda *count: pltpu.SemaphoreType.DMA(count)
-    plane, groups, ring = n * n, 2 * n, n * cb
     vm = pl.BlockSpec(memory_space=pltpu.VMEM)
     hbm = pl.BlockSpec(memory_space=pltpu.HBM)
     x, u, zown, gap = pl.pallas_call(
@@ -559,23 +599,34 @@
             pltpu.VMEM((slots + 1, targets, blk), f32),
             pltpu.VMEM(vec, f32), pltpu.VMEM(vec, f32), pltpu.VMEM(vec, f32),
             pieces(subs, shards), pieces(subs, shards),
-            pieces(subs + 1, plane * cb), pieces(subs + 1, plane * cb),
-            pieces(subs + 1, ring), pieces(subs + 1, ring),
+            pieces(subs, plane * cb), pieces(subs, plane * cb),
+            pieces(subs, ring), pieces(subs, ring),
             pieces(subs, ring), pieces(subs, plane * cb),
-            pieces(subs, shards), pieces(subs, shards),
-            pltpu.VMEM((3, shards, blk), f32), pieces(3, shards),
-            pieces(cb), pieces(3, groups),
+            pieces(subs, shards),
+            pieces(KINDS, groups), pieces(KINDS, shards),
+            pieces(cb), pieces(3, groups), pieces(2, n),
             dma(4), dma(subs), dma(subs),
-            dma(subs + 1), dma(subs + 1), dma(subs + 1), dma(subs + 1),
+            dma(subs), dma(subs), dma(subs), dma(subs),
             dma(subs), dma(subs), dma(subs), dma(subs), dma(subs), dma(subs),
-            dma(3), dma(3), dma(3), dma(3),
+            dma(KINDS), dma(KINDS), dma(3), dma(3), dma(2), dma(2),
         ],
         compiler_params=pltpu.CompilerParams(
             vmem_limit_bytes=VMEM_MIB * MIB, has_side_effects=True, collective_id=0
         ),
         name="admm",
     )(table, tags, tile_data, obs, x, u)
-    primal_gap = gap[0, :targets]
+    x, u, zown, primal_gap = pl.pallas_call(
+        deliver_kernel,
+        out_shape=(
+            shape(vec, f32), shape(vec, f32), shape((cb, targets, blk), f32),
+            shape((targets,), f32),
+        ),
+        in_specs=[vm] * 4,
+        out_specs=(hbm, hbm, hbm, vm),
+        scratch_shapes=[dma(3)],
+        compiler_params=pltpu.CompilerParams(vmem_limit_bytes=MIB),
+        name="deliver",
+    )(x, u, zown, gap)
     return (jnp.swapaxes(x, 1, 2), jnp.swapaxes(u, 1, 2), jnp.swapaxes(zown, 1, 2), primal_gap)
 
 

time: 212 us -> 175 us (0.83)
  Pallas kernels: 197 us -> 167 us
  local copies, waits for them, and re-layouts: 8.52 us -> 1.4 us
    pallas_call x1, Pallas kernels: 197 us -> 164 us  [on_device(): pl.pallas_call(functools.partial(kernel, n, cb, shards * local_cols * blk...]
    unnamed x7 -> x2, local copies, waits for them, and re-layouts: 5.29 us -> 1.22 us
    pallas_call x0 -> x1, Pallas kernels: none -> 2.57 us  [on_device(): pl.pallas_call(deliver_kernel, out_shape=(shape(vec, f32), shape(vec, f32...]
where the time goes in v1:
time: 175 us; the launch traced here: 174 us
  Pallas kernels  167 us (95%)
  other arithmetic  4.55 us (3%)
    pallas_call x1, Pallas kernels, on_device(): pl.pallas_call(functools.partial(kernel, n, cb, shards * local_cols * blk...  164 us

profile of v1, /device:TPU:1, one launch (start us, length us, event | category | flops | bytes accessed | tf_op | source)
XLA Modules:
  0.0 174.4 jit_solution(10097666646378906995)
XLA Ops:
  1.3 0.9 select_reduce_fusion.2
  2.3 0.1 select_reduce_fusion
  2.4 0.7 iota_add_fusion
  3.1 0.7 add_bitcast_fusion
  3.8 0.2 convert_reduce_fusion
  4.0 0.2 convert_reduce_fusion.3
  4.2 0.8 select_reduce_fusion.3
  5.1 0.8 select_reduce_fusion.6
  5.9 0.1 convert_reduce_fusion.4
  6.1 0.1 convert_element_type.48
  6.2 0.0 copy-start
  6.2 1.2 copy-done
  7.4 164.4 %admm.1 = (f32[64,64,128]{2,1,0:T(8,128)S(1)}, f32[64,64,128]{2,1,0:T(8,128)S(1)}, f32[4,64,128]{2,1,0:T(8,128)S(1)}, f32[8,128]{1,0:T(8,128)S(1)}) custom-call(s32[16,128]{1,0:T(8,128)S(1)} %concatenate.3.tab, f32[4,8,8,128]{3,2,1,0:T(8,128)S(1)} %broadcast_in_dim.166.tags_ref, f32[64,128,128]{2,1,0:T(8,128)} %tile_hbm.1, f32[32,64,128]{2,1,0:T(8,128)S(1)} %bitcast.82, ...), custom_call_target="tpu_custom_call" | custom-call | tf_op jit(solution)/shard_map/admm/pallas_call | solution.py:583
  171.8 2.6 %deliver.1 = (f32[64,64,128]{2,1,0:T(8,128)}, f32[64,64,128]{2,1,0:T(8,128)}, f32[4,64,128]{2,1,0:T(8,128)}, f32[64]{0:T(128)}) custom-call(f32[64,64,128]{2,1,0:T(8,128)S(1)} %get-tuple-element.12.x_ref, f32[64,64,128]{2,1,0:T(8,128)S(1)} %get-tuple-element.13.u_ref, f32[4,64,128]{2,1,0:T(8,128)S(1)} %get-tuple-element.14.z_ref, ...), custom_call_target="tpu_custom_call" | custom-call | tf_op jit(solution)/shard_map/deliver/pallas_call | solution.py:618
  (21 shorter events, 0.2 us)
Async XLA Ops:
  6.2 1.2 copy-start

commit v2 on v1

--- a/solution.py
+++ b/solution.py
@@ -46,16 +46,17 @@
 
 def kernel(
     n, cb, mean_of,
-    tab, tags_ref, tile_hbm, obs_hbm, x_hbm, u_hbm,
+    raw_ref, tile_hbm, obs_hbm, x_hbm, u_hbm,
     x_ref, u_ref, zown_ref, gap_ref,
-    tile_ref, obs_ref, fwd_ref, bwd_ref, pb_ref, wb_ref, wseg, qseg, r_ref, p_ref, zu_ref,
+    lists, tab, tags_ref, tile_ref, fwd_ref, bwd_ref, pb_ref, wb_ref, wseg, qseg, r_ref, p_ref, zu_ref,
     box, in1, sum1, in2, sum2, in3, zz2, zz1, zbox, tagin, tagx, share_ref, gin, cin,
-    load_sem, r1_s, r1_r, r2_s, r2_r, r3_s, r3_r, b3_s, b3_r, b2_s, b2_r, b1_s, b1_r,
+    load_sem, tab_sem, r1_s, r1_r, r2_s, r2_r, r3_s, r3_r, b3_s, b3_r, b2_s, b2_r, b1_s, b1_r,
     tag_s, tag_r, gap_s, gap_r, cnt_s, cnt_r,
 ):
     slots, blk, _ = tile_ref.shape
     local_cols, targets, _ = x_ref.shape
-    row_blocks = obs_ref.shape[0]
+    row_blocks = obs_hbm.shape[0]
+    obs_ref = zu_ref.at[pl.ds(0, row_blocks)]
     subs = targets // PIECE
     plane = n * n
     groups = 2 * n
@@ -130,8 +131,84 @@
             ((x_hbm, x_ref), (u_hbm, u_ref), (tile_hbm, tile_ref), (obs_hbm, obs_ref))
         )
     ]
-    for one in loads:
-        one.start()
+    loads[0].start()
+    loads[1].start()
+
+    def line_of(row):
+        return raw_ref[pl.ds(row, 1)].astype(f32)
+
+    def spread(row):
+        return jnp.broadcast_to(row, (blk, blk))
+
+    def flip(row):
+        return spread(row).T
+
+    def tell(row, value):
+        lists[pl.ds(row, 1)] = jnp.clip(value, 0.0, float(blk - 1)).astype(jnp.int32)
+
+    def find(row, at_most, column):
+        return jnp.clip(tab[row, column], 0, at_most)
+
+    def publish(half):
+        part = pl.ds(half * PIECE, PIECE)
+        return pltpu.make_async_copy(lists.at[part], tab.at[part], tab_sem.at[half])
+
+    down = lax.broadcasted_iota(jnp.int32, (blk, blk), 0).astype(f32)
+    across = lax.broadcasted_iota(jnp.int32, (blk, blk), 1).astype(f32)
+    none = jnp.zeros((blk, blk), f32)
+
+    def place():
+        wanted = flip(line_of(0))
+        found = none
+        for j in range(raw_ref.shape[0] - 4):
+            hit = wanted == across + float(j * blk)
+            found = found + jnp.where(hit, spread(line_of(4 + j)), 0.0)
+        position = jnp.sum(found, axis=1, keepdims=True).astype(jnp.int32)
+        owner = position // cb
+        local_slot = (position % cb).astype(f32)
+        away = {
+            "z": (owner % n + n - at["z"]) % n,
+            "x": ((owner // (2 * n)) % n + n - at["x"]) % n,
+            "y": (owner // (2 * n * n) + n - at["y"]) % n,
+        }
+        core = (owner // n + at["c"]) % 2
+        held = down < float(local_cols)
+        for p, (first, second, third) in enumerate(ORDERS):
+            mail = ((core * n + away[first]) * n + away[second]) * n + away[third]
+            mail = jnp.broadcast_to(mail.astype(f32), (blk, blk))
+            tell(MAIL + p, mail.T[:1])
+            hit = held & (mail == across)
+            tell(SLOT + p, jnp.max(jnp.where(hit, down, 0.0), axis=0, keepdims=True))
+            tag = jnp.max(jnp.where(hit, local_slot + 1.0, 0.0), axis=0, keepdims=True) - 1.0
+            tag = jnp.broadcast_to(tag, (PIECE, blk))
+            for g in range(groups):
+                turned = tag if g == 0 else pltpu.roll(tag, blk - g * plane, 1)
+                tags_ref[p, g] = turned
+
+    def sort_tiles(key_row, from_row, bins, first_table, last_table):
+        count = line_of(3)
+        number = across[:1]
+        keys = jnp.where(number < count, line_of(key_row), float(bins))
+        full = keys * float(blk) + number
+        full_a, full_d = spread(full), flip(full)
+        keys_a, keys_d = spread(keys), flip(keys)
+        rank = jnp.sum(jnp.where(full_a < full_d, 1.0, 0.0), axis=1, keepdims=True)
+        earlier = jnp.where((full_a < full_d) & (keys_a == keys_d), 1.0, 0.0)
+        fresh = jnp.sum(earlier, axis=1, keepdims=True) == 0.0
+        landed = rank == across
+
+        def pick(value):
+            return jnp.sum(jnp.where(landed, value, 0.0), axis=0, keepdims=True)
+
+        tell(first_table, pick(down))
+        tell(first_table + 1, pick(flip(line_of(from_row))))
+        tell(first_table + 2, pick(jnp.where(fresh, 1.0, none)))
+        upto = jnp.sum(jnp.where(keys_d <= across, 1.0, 0.0), axis=0, keepdims=True)
+        some = jnp.sum(jnp.where(keys_d == across, 1.0, 0.0), axis=0, keepdims=True)
+        tell(last_table, jnp.where(some > 0.0, upto - 1.0, float(slots)))
+
+    place()
+    publish(0).start()
 
     def members(p):
         return [k for k in range(subs) if order(k) == p]
@@ -140,7 +217,7 @@
         def one(i, carry):
             for g in range(groups):
                 q = g * plane + i
-                slot = tab[SLOT + p, q]
+                slot = find(SLOT + p, local_cols - 1, q)
                 for k in members(p):
                     rows = pl.ds(k * PIECE, PIECE)
                     box[k, q] = x_ref[slot, rows] + u_ref[slot, rows]
@@ -148,7 +225,12 @@
 
         lax.fori_loop(0, plane, one, 0)
 
+    built = set()
+
     def send_r1(k):
+        if order(k) not in built:
+            built.add(order(k))
+            build(order(k))
         line_sends(k, order(k), box, in1, *r1)
 
     def send_r2(k):
@@ -225,12 +307,9 @@
         lax.fori_loop(0, plane, one, 0, unroll=2)
         line_sends(k, p, box, zbox, *b1)
 
-    def start_exchange():
-        for p in range(KINDS):
-            build(p)
-
     def exchange(plan, works):
         tasks = (send_r1, t1, t2, t3, t4, t5)
+        built.clear()
         for step in plan:
             level, k = divmod(step, 10)
             if level == 9:
@@ -247,12 +326,12 @@
             left(box, k, plane, b1)
 
     def tile_pass(tiles_ref, from_row, first_row, source_ref, seg_ref):
-        group = min(16, slots)
+        group = min(32, slots)
 
         def step(number, total):
             for inner in range(group):
                 t = number * group + inner
-                lhs = source_ref[tab[from_row, t]]
+                lhs = source_ref[find(from_row, source_ref.shape[0] - 1, t)]
                 out = jnp.dot(
                     jnp.concatenate([lhs, lhs], axis=1), tiles_ref[t],
                     preferred_element_type=f32,
@@ -279,7 +358,9 @@
 
     loads[0].wait()
     loads[1].wait()
-    start_exchange()
+    loads[2].start()
+    loads[3].start()
+    publish(0).wait()
     pl.semaphore_wait(barrier, len(greeted))
     for p in range(KINDS):
         for dc, da in line:
@@ -303,6 +384,9 @@
         return total
 
     def learn():
+        sort_tiles(1, 2, row_blocks, FWD_TILE, ROW_LAST)
+        sort_tiles(2, 1, local_cols, BWD_TILE, COL_LAST)
+        publish(1).start()
         for p in range(KINDS):
             tagin[p, 0] = tags_ref[p, 0]
             arrived(tagin, p, 1, tagged)
@@ -335,10 +419,11 @@
 
         loop(local_cols, opening)
         loads[2].wait()
+        publish(1).wait()
 
         def convert(t, carry):
-            fwd_ref[t] = split(tile_ref[tab[FWD_TILE, t]].T)
-            bwd_ref[t] = split(tile_ref[tab[BWD_TILE, t]])
+            fwd_ref[t] = split(tile_ref[find(FWD_TILE, slots - 1, t)].T)
+            bwd_ref[t] = split(tile_ref[find(BWD_TILE, slots - 1, t)])
             return carry
 
         loop(slots, convert)
@@ -350,7 +435,7 @@
         loads[3].wait()
 
         def against(r, carry):
-            wb_ref[r] = split(obs_ref[r] - wseg[tab[ROW_LAST, r]])
+            wb_ref[r] = split(obs_ref[r] - wseg[find(ROW_LAST, slots, r)])
             return carry
 
         loop(row_blocks, against)
@@ -363,7 +448,7 @@
         backward()
 
         def one(c, carry):
-            r_ref[c] = qseg[tab[COL_LAST, c]] - COUPLING * x_ref[c]
+            r_ref[c] = qseg[find(COL_LAST, slots, c)] - COUPLING * x_ref[c]
             return carry
 
         loop(local_cols, one)
@@ -399,7 +484,7 @@
         def begin(c, carry):
             rr, gap = carry
             z = jnp.concatenate(
-                [zbox[k, tab[MAIL + order(k), c]] for k in range(subs)], axis=0
+                [zbox[k, find(MAIL + order(k), zbox.shape[1] - 1, c)] for k in range(subs)], axis=0
             )
             d = x_ref[c] - z
             u = u_ref[c] + d
@@ -432,7 +517,7 @@
             forward()
 
             def image(i, ww):
-                w = wseg[tab[ROW_LAST, i]]
+                w = wseg[find(ROW_LAST, slots, i)]
                 if not (last and closing):
                     wb_ref[i] = split(w)
                 return ww + w * w
@@ -448,13 +533,11 @@
                 loop(local_cols, finish)
                 if last:
                     break
-                start_exchange()
-
                 def rest_of_step():
                     backward()
 
                     def close(c, carry):
-                        q = qseg[tab[COL_LAST, c]] + COUPLING * p_ref[c]
+                        q = qseg[find(COL_LAST, slots, c)] + COUPLING * p_ref[c]
                         r_ref[c] = r_ref[c] - size * q - COUPLING * zu_ref[c]
                         return carry
 
@@ -468,7 +551,7 @@
                 gap_send(step + 1)
 
             def reduce(c, total):
-                q = qseg[tab[COL_LAST, c]] + COUPLING * p_ref[c]
+                q = qseg[find(COL_LAST, slots, c)] + COUPLING * p_ref[c]
                 r = r_ref[c] - size * q
                 r_ref[c] = r
                 return total + r * r
@@ -484,7 +567,7 @@
                 pb_ref[c] = split(p)
                 return total + p * p
 
-            pp = lanes(loop(local_cols, direct, zero, unroll=2))
+            pp = lanes(loop(local_cols, direct, zero))
             rr = norm
     gap_ref[...] = jnp.sqrt(gap_total(2) / mean_of)
 
@@ -519,56 +602,15 @@
     assert nd == 2 * n * n and shards == 128 and subs == len(SUB_ORDER)
     assert max(local_cols, slots, row_blocks) <= blk and targets % PIECE == 0
 
-    md, mk = lax.axis_index(AXES[0]), lax.axis_index(AXES[1])
-    wanted = touched[0]
-    matches = wanted[:, None] == jnp.arange(col_blocks, dtype=i32)[None, :]
-    position = jnp.sum(jnp.where(matches, owner_map[None, :], 0), axis=1)
-    owner = position // cb
-    local_slot = position - owner * cb
-    away = {
-        "z": (owner % n - mk) % n,
-        "x": ((owner // (2 * n)) % n - (md // 2) % n) % n,
-        "y": (owner // (2 * n * n) - md // (2 * n)) % n,
-    }
-    core = (owner // n + md) % 2
-    mail = jnp.stack(
-        [((core * n + away[a]) * n + away[b]) * n + away[c] for a, b, c in ORDERS]
-    )
-    hit = mail[:, :, None] == jnp.arange(shards, dtype=i32)[None, None, :]
-    column = jnp.arange(local_cols, dtype=i32)
-    slot_of = jnp.sum(jnp.where(hit, column[None, :, None], 0), axis=1)
-    tags = jnp.sum(jnp.where(hit, local_slot[None, :, None] + 1, 0), axis=1) - 1
-    tags = tags.astype(f32).reshape(KINDS, groups, 1, plane)
-    tags = jnp.pad(tags, ((0, 0), (0, 0), (0, 0), (0, blk - plane)))
-    tags = jnp.broadcast_to(tags, (KINDS, groups, PIECE, blk))
-
-    number = jnp.arange(slots, dtype=i32)
-    used = number < tile_count[0]
-
-    def sorting(keys, values, bins):
-        keys = jnp.where(used, keys, bins)
-        full = keys * slots + number
-        before = full[None, :] < full[:, None]
-        rank = jnp.sum(before.astype(i32), axis=1)
-        same = before & (keys[None, :] == keys[:, None])
-        first = 1 - jnp.max(same.astype(i32), axis=1)
-        landed = rank[None, :] == number[:, None]
-        pick = lambda v: jnp.sum(jnp.where(landed, v[None, :], 0), axis=1)
-        bin_of = jnp.arange(bins, dtype=i32)
-        upto = jnp.sum((keys[None, :] <= bin_of[:, None]).astype(i32), axis=1)
-        some = jnp.max((keys[None, :] == bin_of[:, None]).astype(i32), axis=1)
-        return pick(number), pick(values), pick(first), jnp.where(some > 0, upto - 1, slots)
-
-    row, col = tile_row[0], tile_col[0]
-    ftile, ffrom, ffirst, row_last = sorting(row, col, row_blocks)
-    btile, bfrom, bfirst, col_last = sorting(col, row, local_cols)
-
     def padded(v):
-        return jnp.pad(v, (0, blk - v.shape[0]))[None, :]
-
-    table = jnp.concatenate(
-        [slot_of, jnp.pad(mail, ((0, 0), (0, blk - local_cols)))]
-        + [padded(v) for v in (ftile, ffrom, ffirst, btile, bfrom, bfirst, row_last, col_last)],
+        return jnp.pad(v, ((0, 0), (0, blk - v.shape[1])), constant_values=-1)
+
+    raw = jnp.concatenate(
+        [
+            padded(touched), padded(tile_row), padded(tile_col),
+            jnp.broadcast_to(tile_count[:, None], (1, blk)),
+            owner_map.reshape(-1, blk),
+        ],
         axis=0,
     )
 
@@ -586,11 +628,12 @@
             shape(vec, f32), shape(vec, f32), shape((cb, targets, blk), f32),
             shape((PIECE, blk), f32),
         ),
-        in_specs=[pl.BlockSpec(memory_space=pltpu.SMEM), vm, hbm, hbm, hbm, hbm],
+        in_specs=[vm, hbm, hbm, hbm, hbm],
         out_specs=(vm,) * 4,
         scratch_shapes=[
+            pltpu.VMEM((2 * PIECE, blk), i32), pltpu.SMEM((2 * PIECE, blk), i32),
+            pieces(KINDS, groups),
             pltpu.VMEM((slots, blk, blk), f32),
-            pltpu.VMEM((row_blocks, targets, blk), f32),
             pltpu.VMEM((slots, 2 * blk, blk), b16),
             pltpu.VMEM((slots, 2 * blk, blk), b16),
             pltpu.VMEM((local_cols, 2 * targets, blk), b16),
@@ -605,7 +648,7 @@
             pieces(subs, shards),
             pieces(KINDS, groups), pieces(KINDS, shards),
             pieces(cb), pieces(3, groups), pieces(2, n),
-            dma(4), dma(subs), dma(subs),
+            dma(4), dma(2), dma(subs), dma(subs),
             dma(subs), dma(subs), dma(subs), dma(subs),
             dma(subs), dma(subs), dma(subs), dma(subs), dma(subs), dma(subs),
             dma(KINDS), dma(KINDS), dma(3), dma(3), dma(2), dma(2),
@@ -614,7 +657,7 @@
             vmem_limit_bytes=VMEM_MIB * MIB, has_side_effects=True, collective_id=0
         ),
         name="admm",
-    )(table, tags, tile_data, obs, x, u)
+    )(raw, tile_data, obs, x, u)
     x, u, zown, primal_gap = pl.pallas_call(
         deliver_kernel,
         out_shape=(

time: 175 us -> 165 us (0.943)
  Pallas kernels: 167 us -> 160 us
  other arithmetic: 4.55 us -> 0 us
  local copies, waits for them, and re-layouts: 1.4 us -> 3.91 us
    pallas_call x1, Pallas kernels: 164 us -> 157 us  [on_device(): pl.pallas_call(functools.partial(kernel, n, cb, shards * local_cols * blk...]
    reduce_sum x6 -> x0, other arithmetic: 2.91 us -> none  [the longest x2 1.62 us: sorting(): pick = lambda v: jnp.sum(jnp.where(landed, v[None, :], 0), axis=1)]
    pad x1 -> x3, local copies, waits for them, and re-layouts: 0.01 us -> 1.98 us  [padded(): return jnp.pad(v, ((0, 0), (0, blk - v.shape[1])), constant_values=-1)]
where the time goes in v2:
time: 165 us
  Pallas kernels  160 us (97%)
  local copies, waits for them, and re-layouts  3.91 us (2%)
    pallas_call x1, Pallas kernels, on_device(): pl.pallas_call(functools.partial(kernel, n, cb, shards * local_cols * blk...  157 us

profile of v2, /device:TPU:1, one launch (start us, length us, event | category | flops | bytes accessed | tf_op | source)
XLA Modules:
  0.0 165.2 jit_solution(1083088417124175989)
XLA Ops:
  1.3 0.7 pad.11
  1.9 0.7 pad.12
  2.6 0.7 pad.10
  3.3 0.7 concatenate.3.raw_ref
  4.0 0.0 copy-start
  4.0 1.2 copy-done
  5.2 157.3 %admm.1 = (f32[64,64,128]{2,1,0:T(8,128)S(1)}, f32[64,64,128]{2,1,0:T(8,128)S(1)}, f32[4,64,128]{2,1,0:T(8,128)S(1)}, f32[8,128]{1,0:T(8,128)S(1)}) custom-call(s32[8,128]{1,0:T(8,128)S(1)} %concatenate.3.raw_ref, f32[64,128,128]{2,1,0:T(8,128)} %tile_hbm.1, f32[32,64,128]{2,1,0:T(8,128)S(1)} %bitcast.9, f32[64,64,128]{2,1,0:T(8,128)} %bitcast.10, ...), custom_call_target="tpu_custom_call" | custom-call | tf_op jit(solution)/shard_map/admm/pallas_call | solution.py:625
  162.5 2.6 %deliver.1 = (f32[64,64,128]{2,1,0:T(8,128)}, f32[64,64,128]{2,1,0:T(8,128)}, f32[4,64,128]{2,1,0:T(8,128)}, f32[64]{0:T(128)}) custom-call(f32[64,64,128]{2,1,0:T(8,128)S(1)} %get-tuple-element.12.x_ref, f32[64,64,128]{2,1,0:T(8,128)S(1)} %get-tuple-element.13.u_ref, f32[4,64,128]{2,1,0:T(8,128)S(1)} %get-tuple-element.14.z_ref, ...), custom_call_target="tpu_custom_call" | custom-call | tf_op jit(solution)/shard_map/deliver/pallas_call | solution.py:661
  (1 shorter events, 0.0 us)
Async XLA Ops:
  4.0 1.2 copy-start
